TPU v7x, 32 devices: a whole 2x2x4 slice. The times are simulated.
32 devices in a mesh: blk: 16 (over z, y, x), obs: 2 (over core).
Axes of the slice: x: 2, y: 2, z: 4, core: 2. Of those that a mesh axis runs over, the one named last changes fastest.
Arguments:
- populations: float32 [16, 19, 32, 1024], P('blk', None, 'obs'), may hold values from 0.011111111 to 0.533333333, as said below
- block_faces: int32 [16, 4], P('blk'), may hold values from 0 to 15, as said below
- block_edges: int32 [16, 4], P('blk'), may hold values from 0 to 15, as said below
- probe_cell: int32 [4096], P(('blk', 'obs')), may hold values from 0 to 16383
- history: bfloat16 [4096, 512], P(('blk', 'obs')), may hold values from -6 to 6
- panel_count: int32 [32], P(('blk', 'obs')), may hold values from 0 to 128, as said below
- panel_owner: int32 [4096], P(('blk', 'obs')), may hold values from 0 to 1023, as said below
- panel_pos: bfloat16 [3, 2048], P(None, ('blk', 'obs')), may hold values from -1 to 1
- panel_normal: bfloat16 [3, 2048], P(None, ('blk', 'obs')), may hold values from -0.625 to 0.625
- observers: float32 [3, 1024], P(None, 'obs'), may hold values from -8 to 8, as said below
Outputs:
- populations_out: float32 [16, 19, 32, 1024], P('blk', None, 'obs')
- spectrum: float32 [2, 512, 128], P('obs', 'blk')
Inputs may be any that keep to these rules, and one draw needn't show every extreme that they name: `populations`: every population is positive. The blocks form a lattice of 4 by 4 blocks along y and z, periodic in both, one block deep in x; block_faces[b] names the blocks beside b at -y, +y, -z, +z. block_edges[b] names the blocks at (-y,-z), (-y,+z), (+y,-z), (+y,+z) of b: the y neighbour's z neighbour, which is the z neighbour's y neighbour. The eight face and edge neighbours of a block are distinct and differ from it. The live slots of a device are its first panel_count slots. The counts of the devices at one obs index sum to 1024. `panel_owner`: in a live slot of the device at blk index b and obs index o the value is q * 64 + j: slot j of the owner at blk index q and the same obs index. Every owner slot receives exactly one live panel. A device sends at most 8 live panels to one owner, and its live panels go to the owners in numbers that differ by at most one. Dead slots hold arbitrary values of the range. `observers`: every observer lies at a distance of 4 to 8 from the anchor (0, 0, 0).
All inputs are finite; a program needn't handle non-finite values.
Results may differ from a plain program's by a relative error of at most 0.0032.
The roundings to bfloat16 on the way count: a program that leaves them out, or rounds other values in their place, can miss the bound.
Values may be sent and summed in bfloat16 or wider, within the bound.
A program may use at most 128 MiB of HBM per device.

v0:
```python
import math
import jax
import jax.numpy as jnp
from jax import lax
from jax.sharding import PartitionSpec as P

BS = 32
STEPS = 4
SAMPLES = 256
BINS = 64
P_OWN = 64
velocity_list = [
    (0, 0, 0),
    (1, 0, 0),
    (-1, 0, 0),
    (0, 1, 0),
    (0, -1, 0),
    (0, 0, 1),
    (0, 0, -1),
    (1, 1, 0),
    (-1, -1, 0),
    (1, -1, 0),
    (-1, 1, 0),
    (1, 0, 1),
    (-1, 0, -1),
    (1, 0, -1),
    (-1, 0, 1),
    (0, 1, 1),
    (0, -1, -1),
    (0, 1, -1),
    (0, -1, 1),
]
weight_list = [1.0 / 3.0] + [1.0 / 18.0] * 6 + [1.0 / 36.0] * 12
x_moving = [1, 2, 7, 8, 9, 10, 11, 12, 13, 14]
y_upward = [3, 7, 10, 15, 17]
y_downward = [4, 8, 9, 16, 18]
z_upward = [5, 11, 14, 15, 18]
z_downward = [6, 12, 13, 16, 17]
relax_rate = 1.6
pressure_gain = 60.0
sound_speed = 0.5


def padded(block, sides, width):
    for axis, dim in sides:
        count = lax.axis_size(axis)
        forward = [(i, i + 1) for i in range(count - 1)]
        forward.append((count - 1, 0))
        backward = [(target, source) for source, target in forward]
        low = lax.ppermute(
            lax.slice_in_dim(block, block.shape[dim] - width, None, axis=dim), axis, forward
        )
        high = lax.ppermute(lax.slice_in_dim(block, 0, width, axis=dim), axis, backward)
        block = jnp.concatenate([low, block, high], axis=dim)
    return block


def component(axis_number, extra):
    values = jnp.array([velocity[axis_number] for velocity in velocity_list], jnp.float32)
    return values.reshape((19,) + extra)


def collide(field):
    extra = (1,) * (field.ndim - 1)
    along_x = component(0, extra)
    along_y = component(1, extra)
    along_z = component(2, extra)
    weights = jnp.array(weight_list, jnp.float32).reshape((19,) + extra)
    density = jnp.sum(field, axis=0)
    speed_x = jnp.sum(along_x * field, axis=0) / density
    speed_y = jnp.sum(along_y * field, axis=0) / density
    speed_z = jnp.sum(along_z * field, axis=0) / density
    projected = along_x * speed_x + along_y * speed_y + along_z * speed_z
    squared = speed_x * speed_x + speed_y * speed_y + speed_z * speed_z
    equilibrium = (
        weights * density * (1.0 + 3.0 * projected + 4.5 * projected * projected - 1.5 * squared)
    )
    return field + relax_rate * (equilibrium - field)


def stream_merged(widened, planes):
    below_plane, above_plane, near_plane, far_plane = planes
    slab_depth = widened.shape[1] - 2
    lane_count = widened.shape[2]
    lane_index = jnp.arange(lane_count, dtype=jnp.int32)
    lane_row = lane_index // BS
    lane_column = lane_index % BS
    parts = []
    for number, velocity in enumerate(velocity_list):
        shift_x, shift_y, shift_z = velocity
        begin = 1 - shift_x
        moved = jnp.roll(
            widened[number, begin : begin + slab_depth], shift_y * BS + shift_z, axis=-1
        )
        if shift_y != 0:
            source_plane = below_plane if shift_y == 1 else above_plane
            row_values = jnp.roll(
                source_plane[number, begin : begin + slab_depth], shift_z, axis=-1
            )
            edge_index = 0 if shift_y == 1 else BS - 1
            moved = jnp.where(
                (lane_row == edge_index)[None, :], jnp.tile(row_values, (1, BS)), moved
            )
        if shift_z != 0:
            source_plane = near_plane if shift_z == 1 else far_plane
            column_values = source_plane[
                number, begin : begin + slab_depth, 1 - shift_y : 1 - shift_y + BS
            ]
            edge_index = 0 if shift_z == 1 else BS - 1
            moved = jnp.where(
                (lane_column == edge_index)[None, :], jnp.repeat(column_values, BS, axis=-1), moved
            )
        parts.append(moved)
    return jnp.stack(parts)


def place_pieces(pieces, targets, blocks):
    onehot = (targets[:, None] == jnp.arange(blocks, dtype=jnp.int32)[None, :]).astype(jnp.float32)
    return jnp.einsum("kn,kf->nf", onehot, pieces, precision=lax.Precision.HIGHEST)


def spread_pops(piece, chosen, shape):
    return jnp.zeros(shape, jnp.float32).at[jnp.array(chosen)].set(piece)


def direct_halo(widened, block_faces, block_edges, blocks):
    depth_x = widened.shape[1]
    lane_count = widened.shape[2]

    def corner_piece(number, lane_at):
        return jnp.zeros((5, depth_x, BS), jnp.float32).at[0, :, 0].set(widened[number, :, lane_at])

    def corner_plane(number, vector):
        return jnp.zeros((19, depth_x, 1), jnp.float32).at[number, :, 0].set(vector)

    outgoing = jnp.stack(
        [
            widened[jnp.array(y_downward), :, 0:BS],
            widened[jnp.array(y_upward), :, lane_count - BS :],
            widened[jnp.array(z_downward), :, 0::BS],
            widened[jnp.array(z_upward), :, BS - 1 :: BS],
            corner_piece(16, 0),
            corner_piece(18, BS - 1),
            corner_piece(17, (BS - 1) * BS),
            corner_piece(15, BS * BS - 1),
        ]
    ).reshape(8, -1)
    targets = jnp.concatenate([block_faces, block_edges])
    received = lax.all_to_all(
        place_pieces(outgoing, targets, blocks), "blk", split_axis=0, concat_axis=0, tiled=True
    )
    chosen = jnp.take(received, targets, axis=0).reshape(8, 5, depth_x, BS)
    below_plane = spread_pops(chosen[0], y_upward, (19, depth_x, BS))
    above_plane = spread_pops(chosen[1], y_downward, (19, depth_x, BS))
    near_core = spread_pops(chosen[2], z_upward, (19, depth_x, BS))
    far_core = spread_pops(chosen[3], z_downward, (19, depth_x, BS))
    near_plane = jnp.concatenate(
        [corner_plane(15, chosen[4, 0, :, 0]), near_core, corner_plane(18, chosen[6, 0, :, 0])],
        axis=2,
    )
    far_plane = jnp.concatenate(
        [corner_plane(17, chosen[5, 0, :, 0]), far_core, corner_plane(16, chosen[7, 0, :, 0])],
        axis=2,
    )
    return (below_plane, above_plane, near_plane, far_plane)


def transform_table():
    moments = jnp.arange(SAMPLES, dtype=jnp.int32)[:, None]
    harmonics = jnp.arange(BINS, dtype=jnp.int32)[None, :] + 1
    turns = moments * harmonics % SAMPLES
    phases = turns.astype(jnp.float32) * (2.0 * math.pi / SAMPLES)
    return jnp.concatenate([jnp.cos(phases), -jnp.sin(phases)], axis=1).astype(jnp.bfloat16)


def radiate(spectra, place, normal, listen):
    values = spectra.astype(jnp.float32)
    press_real = values[0:BINS].T
    press_imag = values[BINS : 2 * BINS].T
    rate_real = values[2 * BINS : 3 * BINS].T
    rate_imag = values[3 * BINS : 4 * BINS].T
    offsets = listen[:, None, :] - place.astype(jnp.float32)[:, :, None]
    distance_sq = jnp.sum(offsets * offsets, axis=0)
    distance = jnp.sqrt(distance_sq)
    facing = jnp.sum(normal.astype(jnp.float32)[:, :, None] * offsets, axis=0)
    far_term = facing / (4.0 * math.pi * sound_speed * distance_sq)
    near_term = facing / (4.0 * math.pi * distance_sq * distance)
    angular = (jnp.arange(BINS, dtype=jnp.float32) + 1.0) * (2.0 * math.pi / SAMPLES)
    phases = angular[None, :, None] * (distance / sound_speed)[:, None, :]
    cosine = jnp.cos(phases)
    sine_part = jnp.sin(phases)
    weight_real = (
        far_term[:, None, :] * rate_real[:, :, None]
        + near_term[:, None, :] * press_real[:, :, None]
    )
    weight_imag = (
        far_term[:, None, :] * rate_imag[:, :, None]
        + near_term[:, None, :] * press_imag[:, :, None]
    )
    real_part = jnp.sum(weight_real * cosine + weight_imag * sine_part, axis=0)
    imag_part = jnp.sum(weight_imag * cosine - weight_real * sine_part, axis=0)
    return jnp.concatenate([real_part, imag_part], axis=0).T


def radiate_blocks(spectra, place, normal, listen):
    count_panels = spectra.shape[1]
    listener_count = listen.shape[1]
    block_size = 128
    while block_size > 1 and (
        count_panels % block_size != 0 or block_size * listener_count > 16384
    ):
        block_size = block_size // 2

    def radiate_accumulate(block_number, total):
        begin = block_number * block_size
        return total + radiate(
            lax.dynamic_slice_in_dim(spectra, begin, block_size, 1),
            lax.dynamic_slice_in_dim(place, begin, block_size, 1),
            lax.dynamic_slice_in_dim(normal, begin, block_size, 1),
            listen,
        )

    return lax.fori_loop(
        0,
        count_panels // block_size,
        radiate_accumulate,
        jnp.zeros((listener_count, 2 * BINS), jnp.float32),
    )


def route_slots(payload, owners, alive_slot, blocks):
    count_slots = payload.shape[0]
    capacity = -(-count_slots // blocks)
    target = owners // P_OWN
    member = (
        (target[:, None] == jnp.arange(blocks, dtype=jnp.int32)[None, :]) & alive_slot[:, None]
    ).astype(jnp.int32)
    before = jnp.cumsum(member, axis=0) - member
    order_within = jnp.sum(before * member, axis=1)
    slot_label = jnp.where(alive_slot, target * capacity + order_within, -1)
    matches = slot_label[:, None] == jnp.arange(blocks * capacity, dtype=jnp.int32)[None, :]
    source = jnp.sum(
        jnp.where(matches, jnp.arange(count_slots, dtype=jnp.int32)[:, None], 0), axis=0
    )
    filled = jnp.any(matches, axis=0)
    outgoing = jnp.take(payload, source, axis=0).reshape(blocks, capacity, payload.shape[1])
    tagged = jnp.where(filled, jnp.take(owners, source), -1).reshape(blocks, capacity)
    return (outgoing, tagged)


def settle(incoming, tagged):
    keeper = lax.axis_index("blk")
    flat_tags = tagged.reshape(-1)
    slot_here = flat_tags - keeper * P_OWN
    choose = (
        (slot_here[:, None] == jnp.arange(P_OWN, dtype=jnp.int32)[None, :])
        & (flat_tags[:, None] >= 0)
    ).astype(jnp.bfloat16)
    return jnp.einsum(
        "rw,rp->wp",
        incoming.reshape(-1, incoming.shape[-1]),
        choose,
        preferred_element_type=jnp.float32,
    ).astype(jnp.bfloat16)


def body(
    populations,
    block_faces,
    block_edges,
    probe_cell,
    history,
    panel_count,
    panel_owner,
    panel_pos,
    panel_normal,
    observers,
):
    blocks = lax.axis_size("blk")
    lattice_state = populations[0]
    slab_depth = lattice_state.shape[1]
    lane_count = lattice_state.shape[2]
    faces_here = block_faces[0]
    edges_here = block_edges[0]
    readings = []
    for turn_index in range(STEPS):
        collided = collide(lattice_state)
        slab_edges = padded(collided[jnp.array(x_moving)], (("obs", 1),), 1)
        lower_plane = spread_pops(slab_edges[:, 0:1], x_moving, (19, 1, lane_count))
        upper_plane = spread_pops(slab_edges[:, -1:], x_moving, (19, 1, lane_count))
        widened = jnp.concatenate([lower_plane, collided, upper_plane], axis=1)
        planes = direct_halo(widened, faces_here, edges_here, blocks)
        lattice_state = stream_merged(widened, planes)
        density = jnp.sum(lattice_state, axis=0).reshape(-1)
        readings.append(jnp.take(density, probe_cell))
    populations_out = lattice_state.reshape(1, 19, slab_depth, lane_count)
    gained = pressure_gain * (jnp.stack(readings, axis=1) - 1.0)
    previous = jnp.concatenate(
        [history[:, SAMPLES - 1 : SAMPLES].astype(jnp.float32), gained[:, :-1]], axis=1
    )
    rate_values = gained - previous
    recent = jnp.concatenate(
        [
            history[:, STEPS:SAMPLES],
            gained.astype(jnp.bfloat16),
            history[:, SAMPLES + STEPS :],
            rate_values.astype(jnp.bfloat16),
        ],
        axis=1,
    )
    transform = transform_table()
    count_slots = recent.shape[0]
    alive_slot = jnp.arange(count_slots, dtype=jnp.int32) < panel_count[0]
    outgoing, tagged = route_slots(recent, panel_owner, alive_slot, blocks)
    incoming, tags_in = (
        lax.all_to_all(outgoing, "blk", split_axis=0, concat_axis=0, tiled=True),
        lax.all_to_all(tagged, "blk", split_axis=0, concat_axis=0, tiled=True),
    )
    histories = settle(incoming, tags_in).reshape(2, SAMPLES, P_OWN)
    spectra = (
        jnp.einsum("tk,gtp->gkp", transform, histories, preferred_element_type=jnp.float32)
        .astype(jnp.bfloat16)
        .reshape(4 * BINS, P_OWN)
    )
    partial_value = radiate_blocks(
        lax.all_gather(spectra, "obs", axis=1, tiled=True),
        lax.all_gather(panel_pos, "obs", axis=1, tiled=True),
        lax.all_gather(panel_normal, "obs", axis=1, tiled=True),
        observers,
    )
    summed = lax.psum_scatter(partial_value, "blk", scatter_dimension=0, tiled=True)
    return (populations_out, summed.reshape(1, -1, 2 * BINS))


def solution(mesh):
    placed = (
        P("blk", None, "obs", None),
        P("blk", None),
        P("blk", None),
        P(("blk", "obs")),
        P(("blk", "obs"), None),
        P(("blk", "obs")),
        P(("blk", "obs")),
        P(None, ("blk", "obs")),
        P(None, ("blk", "obs")),
        P(None, "obs"),
    )
    return jax.shard_map(
        body,
        mesh=mesh,
        in_specs=placed,
        out_specs=(P("blk", None, "obs", None), P("obs", "blk", None)),
        check_vma=False,
    )
```

profile of v0, /device:TPU:0, one launch (start us, length us, event | category | flops | bytes accessed | tf_op | source)
XLA Modules:
  0.0 673.8 jit_solution(10351201009113472713)
XLA Ops:
  21.0 1.9 all-gather.1
  23.0 1.8 all-gather
  56.1 5.3 copy.672
  61.4 7.4 %copy.668 = f32[19,18,1024]{1,0,2:T(8,128)} copy(f32[19,18,1024]{2,1,0:T(8,128)S(1)} %pad_maximum_fusion) | data formatting | bytes 2801664 | tf_op jit(solution)/shard_map/concatenate | solution.py:291
  69.6 2.7 gather_fusion.4
  72.3 2.7 gather_fusion.3
  75.5 1.5 gather_fusion.2
  77.1 1.5 gather_fusion.1
  80.6 8.4 %all-to-all-start = ((f32[16,1,2880]{2,1,0:T(1,128)}), f32[16,1,2880]{2,1,0:T(1,128)S(1)}, u32[]{:S(2)}, u32[]{:S(2)}) async-start(f32[16,1,2880]{2,1,0:T(1,128)} %copy.680), calls=%async_computation | async-start | bytes 376832 | tf_op jit(solution)/shard_map/all_to_all | solution.py:149
  155.4 1.6 select_add_fusion.3
  184.0 5.2 copy.695
  189.2 3.4 gather_fusion.9
  192.6 3.4 gather_fusion.8
  196.0 7.4 %copy.691 = f32[19,18,1024]{1,0,2:T(8,128)} copy(f32[19,18,1024]{2,1,0:T(8,128)S(1)} %pad_maximum_fusion.1) | data formatting | bytes 2801664 | tf_op jit(solution)/shard_map/concatenate | solution.py:291
  203.4 1.5 gather_fusion.7
  204.9 1.5 gather_fusion.6
  209.7 7.3 %all-to-all-start.1 = ((f32[16,1,2880]{2,1,0:T(1,128)}), f32[16,1,2880]{2,1,0:T(1,128)S(1)}, u32[]{:S(2)}, u32[]{:S(2)}) async-start(f32[16,1,2880]{2,1,0:T(1,128)} %copy.703), calls=%async_computation.1 | async-start | bytes 376832 | tf_op jit(solution)/shard_map/all_to_all | solution.py:149
  283.6 1.6 select_add_fusion.2
  285.2 1.8 gather_fusion.27
  312.2 5.2 copy.718
  317.4 3.4 gather_fusion.14
  320.8 3.4 gather_fusion.13
  324.2 7.4 %copy.714 = f32[19,18,1024]{1,0,2:T(8,128)} copy(f32[19,18,1024]{2,1,0:T(8,128)S(1)} %pad_maximum_fusion.2) | data formatting | bytes 2801664 | tf_op jit(solution)/shard_map/concatenate | solution.py:291
  333.1 1.5 gather_fusion.11
  337.9 7.1 %all-to-all-start.2 = ((f32[16,1,2880]{2,1,0:T(1,128)}), f32[16,1,2880]{2,1,0:T(1,128)S(1)}, u32[]{:S(2)}, u32[]{:S(2)}) async-start(f32[16,1,2880]{2,1,0:T(1,128)} %copy.726), calls=%async_computation.2 | async-start | bytes 376832 | tf_op jit(solution)/shard_map/all_to_all | solution.py:149
  411.6 1.6 select_add_fusion.1
  413.2 1.9 gather_fusion.28
  429.7 5.2 copy.741
  434.9 2.7 gather_fusion.19
  437.7 2.7 gather_fusion.18
  440.4 7.4 %copy.737 = f32[19,18,1024]{1,0,2:T(8,128)} copy(f32[19,18,1024]{2,1,0:T(8,128)S(1)} %pad_maximum_fusion.3) | data formatting | bytes 2801664 | tf_op jit(solution)/shard_map/concatenate | solution.py:291
  449.3 1.5 gather_fusion.16
  453.9 6.9 %all-to-all-start.3 = ((f32[16,1,2880]{2,1,0:T(1,128)}), f32[16,1,2880]{2,1,0:T(1,128)S(1)}, u32[]{:S(2)}, u32[]{:S(2)}) async-start(f32[16,1,2880]{2,1,0:T(1,128)} %copy.749), calls=%async_computation.3 | async-start | bytes 376832 | tf_op jit(solution)/shard_map/all_to_all | solution.py:149
  463.5 5.7 all-to-all-done.3
  469.3 4.1 all-to-all-start.5
  485.5 1.6 fusion.114
  487.1 1.6 fusion.113
  489.5 1.6 fusion.111
  491.2 1.6 fusion.110
  505.0 7.0 %all-to-all-start.4 = ((bf16[16,8,512]{2,1,0:T(8,128)(2,1)}), bf16[16,8,512]{2,1,0:T(8,128)(2,1)S(1)}, u32[]{:S(2)}, u32[]{:S(2)}) async-start(bf16[16,8,512]{2,1,0:T(8,128)(2,1)} %bitcast_select_fusion), calls=%async_computation.4 | async-start | bytes 262144 | tf_op jit(solution)/shard_map/all_to_all | solution.py:316
  512.3 7.5 %all-to-all-done.4 = bf16[16,8,512]{2,1,0:T(8,128)(2,1)S(1)} async-done(((bf16[16,8,512]{2,1,0:T(8,128)(2,1)}), bf16[16,8,512]{2,1,0:T(8,128)(2,1)S(1)}, u32[]{:S(2)}, u32[]{:S(2)}) %all-to-all-start.4) | async-done | bytes 131104 | tf_op jit(solution)/shard_map/all_to_all | solution.py:316
  520.3 2.0 all_gather.11
  522.3 69.2 %while.46 = (s32[]{:T(128)}, f32[512,128]{0,1:T(8,128)S(1)}, bf16[3,128]{1,0:T(4,128)(2,1)S(1)}, f32[3,512]{1,0:T(4,128)S(1)}, bf16[3,128]{1,0:T(4,128)(2,1)S(1)...) while((s32[]{:T(128)}, f32[512,128]{0,1:T(8,128)S(1)}, ...), condition=%wide.region_46.49_spmd.clone, body=%wide.region_41.48_spmd.clone.sunk | while | flops 16179527 | bytes 1860141 | solution.py:223
  522.7 16.8 %fusion.295 = (f32[64,512]{1,0:T(8,128)S(1)}, f32[64,512]{1,0:T(8,128)S(1)}) fusion(f32[32,64]{1,0:T(8,128)S(1)} %get-tuple-element.1175, f32[32,64]{1,0:T(8,128)S(1)} %get-tuple-element.1176, f32[32,512]{1,0:T(8,128)S(1)} %get-tuple-element.1181, f32[64]{0:T(128)S(1)} %add_multiply_fusion.3, f32[32,64]{1,0:T(8,128)S(1)} %get-tuple-element.1182, ...), kind=kLoop, calls=%fused_computation.61.clone.1 | loop fusion | flops 15663104 | bytes 491776 | tf_op jit(solution)/shard_map/while/body/eval_jaxpr/reduce_sum | solution.py:200
  540.0 16.8 %fusion.295 = (f32[64,512]{1,0:T(8,128)S(1)}, f32[64,512]{1,0:T(8,128)S(1)}) fusion(f32[32,64]{1,0:T(8,128)S(1)} %get-tuple-element.1175, f32[32,64]{1,0:T(8,128)S(1)} %get-tuple-element.1176, f32[32,512]{1,0:T(8,128)S(1)} %get-tuple-element.1181, f32[64]{0:T(128)S(1)} %add_multiply_fusion.3, f32[32,64]{1,0:T(8,128)S(1)} %get-tuple-element.1182, ...), kind=kLoop, calls=%fused_computation.61.clone.1 | loop fusion | flops 15663104 | bytes 491776 | tf_op jit(solution)/shard_map/while/body/eval_jaxpr/reduce_sum | solution.py:200
  557.3 16.8 %fusion.295 = (f32[64,512]{1,0:T(8,128)S(1)}, f32[64,512]{1,0:T(8,128)S(1)}) fusion(f32[32,64]{1,0:T(8,128)S(1)} %get-tuple-element.1175, f32[32,64]{1,0:T(8,128)S(1)} %get-tuple-element.1176, f32[32,512]{1,0:T(8,128)S(1)} %get-tuple-element.1181, f32[64]{0:T(128)S(1)} %add_multiply_fusion.3, f32[32,64]{1,0:T(8,128)S(1)} %get-tuple-element.1182, ...), kind=kLoop, calls=%fused_computation.61.clone.1 | loop fusion | flops 15663104 | bytes 491776 | tf_op jit(solution)/shard_map/while/body/eval_jaxpr/reduce_sum | solution.py:200
  574.6 16.8 %fusion.295 = (f32[64,512]{1,0:T(8,128)S(1)}, f32[64,512]{1,0:T(8,128)S(1)}) fusion(f32[32,64]{1,0:T(8,128)S(1)} %get-tuple-element.1175, f32[32,64]{1,0:T(8,128)S(1)} %get-tuple-element.1176, f32[32,512]{1,0:T(8,128)S(1)} %get-tuple-element.1181, f32[64]{0:T(128)S(1)} %add_multiply_fusion.3, f32[32,64]{1,0:T(8,128)S(1)} %get-tuple-element.1182, ...), kind=kLoop, calls=%fused_computation.61.clone.1 | loop fusion | flops 15663104 | bytes 491776 | tf_op jit(solution)/shard_map/while/body/eval_jaxpr/reduce_sum | solution.py:200
  592.4 74.4 %reduce-scatter.2.cloned.1.call-done = f32[32,128]{1,0:T(8,128)} async-done(((f32[512,128]{1,0:T(8,128)}), f32[32,128]{1,0:T(8,128)}) %reduce-scatter.2.cloned.1.call-update) | async-done | bytes 16400 | tf_op jit(solution)/shard_map/reduce_scatter | solution.py:331
  (1800 shorter events, 350.6 us)
Async XLA Ops:
  11.5 11.5 %copy-start.426 = (bf16[3,64]{1,0:T(4,128)(2,1)S(1)}, bf16[3,64]{1,0:T(4,128)(2,1)}, u32[]{:S(2)}) copy-start(bf16[3,64]{1,0:T(4,128)(2,1)} %param.148) | copy-start | bytes 1156
  12.2 19.8 %collective-permute-start = (f32[10,1,1024]{2,1,0:T(1,128)S(1)}, f32[10,1,1024]{2,1,0:T(1,128)S(1)}, u32[]{:S(2)}, u32[]{:S(2)}) collective-permute-start(f32[10,1,1024]{2,1,0:T(1,128)S(1)} %get-tuple-element.752), channel_id=1, source_target_pairs={{0,1},{1,0},{2,3},{3,2},{4,5},{5,4},{6,7},{7,6},{8,9},{9,8},{10,11... | collective-permute-start | bytes 122888 | tf_op jit(solution)/shard_map/ppermute | solution.py:50
  12.7 18.4 %collective-permute-start.1 = (f32[10,1,1024]{2,1,0:T(1,128)S(1)}, f32[10,1,1024]{2,1,0:T(1,128)S(1)}, u32[]{:S(2)}, u32[]{:S(2)}) collective-permute-start(f32[10,1,1024]{2,1,0:T(1,128)S(1)} %get-tuple-element.753), channel_id=1, source_target_pairs={{1,0},{0,1},{3,2},{2,3},{5,4},{4,5},{7,6},{6,7},{9,8},{8,9},{11,10... | collective-permute-start | bytes 122888 | tf_op jit(solution)/shard_map/ppermute | solution.py:53
  16.8 14.2 %copy-start.420 = (s32[1024]{0:T(1024)}, s32[1024]{0:T(1024)S(1)}, u32[]{:S(2)}) copy-start(s32[1024]{0:T(1024)S(1)} %get-tuple-element.1095) | copy-start | bytes 12292
  77.0 12.0 %copy-start.161 = (f32[16,992]{1,0:T(8,128)S(1)}, f32[16,992]{1,0:T(8,128)}, u32[]{:S(2)}) copy-start(f32[16,992]{1,0:T(8,128)} %get-tuple-element.1039) | copy-start | bytes 190468
  77.0 12.0 %copy-start.320 = (f32[16,32]{1,0:T(8,128)S(1)}, f32[16,32]{1,0:T(8,128)}, u32[]{:S(2)}) copy-start(f32[16,32]{1,0:T(8,128)} %get-tuple-element.1037) | copy-start | bytes 6148
  77.0 12.1 %copy-start.164 = (f32[16,992]{1,0:T(8,128)S(1)}, f32[16,992]{1,0:T(8,128)}, u32[]{:S(2)}) copy-start(f32[16,992]{1,0:T(8,128)} %get-tuple-element.1045) | copy-start | bytes 190468
  77.0 12.1 %copy-start.323 = (f32[16,32]{1,0:T(8,128)S(1)}, f32[16,32]{1,0:T(8,128)}, u32[]{:S(2)}) copy-start(f32[16,32]{1,0:T(8,128)} %get-tuple-element.1047) | copy-start | bytes 6148
  77.0 12.1 %copy-start.167 = (f32[16,1023]{1,0:T(8,128)S(1)}, f32[16,1023]{1,0:T(8,128)}, u32[]{:S(2)}) copy-start(f32[16,1023]{1,0:T(8,128)} %get-tuple-element.1055) | copy-start | bytes 196420
  77.0 12.1 %copy-start.326 = (f32[16,1]{1,0:T(8,128)S(1)}, f32[16,1]{1,0:T(8,128)}, u32[]{:S(2)}) copy-start(f32[16,1]{1,0:T(8,128)} %get-tuple-element.1053) | copy-start | bytes 196
  77.0 12.2 %copy-start.170 = (f32[16,992]{1,0:T(8,128)S(1)}, f32[16,992]{1,0:T(8,128)}, u32[]{:S(2)}) copy-start(f32[16,992]{1,0:T(8,128)} %get-tuple-element.1041) | copy-start | bytes 190468
  77.1 12.2 %copy-start.329 = (f32[16,32]{1,0:T(8,128)S(1)}, f32[16,32]{1,0:T(8,128)}, u32[]{:S(2)}) copy-start(f32[16,32]{1,0:T(8,128)} %get-tuple-element.1043) | copy-start | bytes 6148
  78.6 10.8 %copy-start.176 = (f32[16,1023]{1,0:T(8,128)S(1)}, f32[16,1023]{1,0:T(8,128)}, u32[]{:S(2)}) copy-start(f32[16,1023]{1,0:T(8,128)} %get-tuple-element.1057) | copy-start | bytes 196420
  78.6 10.8 %copy-start.335 = (f32[16,1]{1,0:T(8,128)S(1)}, f32[16,1]{1,0:T(8,128)}, u32[]{:S(2)}) copy-start(f32[16,1]{1,0:T(8,128)} %get-tuple-element.1059) | copy-start | bytes 196
  78.7 10.8 %copy-start.179 = (f32[16,1023]{1,0:T(8,128)S(1)}, f32[16,1023]{1,0:T(8,128)}, u32[]{:S(2)}) copy-start(f32[16,1023]{1,0:T(8,128)} %get-tuple-element.1067) | copy-start | bytes 196420
  78.7 10.8 %copy-start.338 = (f32[16,1]{1,0:T(8,128)S(1)}, f32[16,1]{1,0:T(8,128)}, u32[]{:S(2)}) copy-start(f32[16,1]{1,0:T(8,128)} %get-tuple-element.1065) | copy-start | bytes 196
  78.7 10.9 %copy-start.184 = (f32[16,1023]{1,0:T(8,128)S(1)}, f32[16,1023]{1,0:T(8,128)}, u32[]{:S(2)}) copy-start(f32[16,1023]{1,0:T(8,128)} %get-tuple-element.1061) | copy-start | bytes 196420
  78.8 10.9 %copy-start.341 = (f32[16,1]{1,0:T(8,128)S(1)}, f32[16,1]{1,0:T(8,128)}, u32[]{:S(2)}) copy-start(f32[16,1]{1,0:T(8,128)} %get-tuple-element.1063) | copy-start | bytes 196
  78.9 10.8 %copy-start.191 = (f32[16,992]{1,0:T(8,128)S(1)}, f32[16,992]{1,0:T(8,128)}, u32[]{:S(2)}) copy-start(f32[16,992]{1,0:T(8,128)} %get-tuple-element.1023) | copy-start | bytes 190468
  78.9 10.8 %copy-start.347 = (f32[16,32]{1,0:T(8,128)S(1)}, f32[16,32]{1,0:T(8,128)}, u32[]{:S(2)}) copy-start(f32[16,32]{1,0:T(8,128)} %get-tuple-element.1021) | copy-start | bytes 6148
  80.6 20.7 %all-to-all-start = ((f32[16,1,2880]{2,1,0:T(1,128)}), f32[16,1,2880]{2,1,0:T(1,128)S(1)}, u32[]{:S(2)}, u32[]{:S(2)}) async-start(f32[16,1,2880]{2,1,0:T(1,128)} %copy.680), calls=%async_computation | async-start | bytes 376832 | tf_op jit(solution)/shard_map/all_to_all | solution.py:149
  90.3 10.9 %copy-start.2 = (f32[19,16,1024]{2,1,0:T(8,128)S(1)}, f32[19,16,1024]{2,1,0:T(8,128)}, u32[]{:S(2)}) copy-start(f32[19,16,1024]{2,1,0:T(8,128)} %get-tuple-element.745) | copy-start | bytes 3735556
  90.3 10.9 %copy-start.77 = (f32[1,16,1024]{2,1,0:T(8,128)S(1)}, f32[1,16,1024]{2,1,0:T(8,128)}, u32[]{:S(2)}) copy-start(f32[1,16,1024]{2,1,0:T(8,128)} %get-tuple-element.702) | copy-start | bytes 196612
  90.4 10.9 %copy-start.75 = (f32[1,16,1024]{2,1,0:T(8,128)S(1)}, f32[1,16,1024]{2,1,0:T(8,128)}, u32[]{:S(2)}) copy-start(f32[1,16,1024]{2,1,0:T(8,128)} %get-tuple-element.701) | copy-start | bytes 196612
  154.7 5.0 collective-permute-start.2
  154.7 4.1 collective-permute-start.3
  209.7 19.7 %all-to-all-start.1 = ((f32[16,1,2880]{2,1,0:T(1,128)}), f32[16,1,2880]{2,1,0:T(1,128)S(1)}, u32[]{:S(2)}, u32[]{:S(2)}) async-start(f32[16,1,2880]{2,1,0:T(1,128)} %copy.703), calls=%async_computation.1 | async-start | bytes 376832 | tf_op jit(solution)/shard_map/all_to_all | solution.py:149
  218.4 11.0 %copy-start.3 = (f32[19,16,1024]{2,1,0:T(8,128)S(1)}, f32[19,16,1024]{2,1,0:T(8,128)}, u32[]{:S(2)}) copy-start(f32[19,16,1024]{2,1,0:T(8,128)} %get-tuple-element.735) | copy-start | bytes 3735556
  218.4 11.0 %copy-start.81 = (f32[1,16,1024]{2,1,0:T(8,128)S(1)}, f32[1,16,1024]{2,1,0:T(8,128)}, u32[]{:S(2)}) copy-start(f32[1,16,1024]{2,1,0:T(8,128)} %get-tuple-element.692) | copy-start | bytes 196612
  218.5 10.9 %copy-start.79 = (f32[1,16,1024]{2,1,0:T(8,128)S(1)}, f32[1,16,1024]{2,1,0:T(8,128)}, u32[]{:S(2)}) copy-start(f32[1,16,1024]{2,1,0:T(8,128)} %get-tuple-element.691) | copy-start | bytes 196612
  282.9 4.9 collective-permute-start.4
  282.9 4.1 collective-permute-start.5
  337.9 19.5 %all-to-all-start.2 = ((f32[16,1,2880]{2,1,0:T(1,128)}), f32[16,1,2880]{2,1,0:T(1,128)S(1)}, u32[]{:S(2)}, u32[]{:S(2)}) async-start(f32[16,1,2880]{2,1,0:T(1,128)} %copy.726), calls=%async_computation.2 | async-start | bytes 376832 | tf_op jit(solution)/shard_map/all_to_all | solution.py:149
  346.4 11.0 %copy-start.4 = (f32[19,16,1024]{2,1,0:T(8,128)S(1)}, f32[19,16,1024]{2,1,0:T(8,128)}, u32[]{:S(2)}) copy-start(f32[19,16,1024]{2,1,0:T(8,128)} %get-tuple-element.725) | copy-start | bytes 3735556
  346.4 11.0 %copy-start.85 = (f32[1,16,1024]{2,1,0:T(8,128)S(1)}, f32[1,16,1024]{2,1,0:T(8,128)}, u32[]{:S(2)}) copy-start(f32[1,16,1024]{2,1,0:T(8,128)} %get-tuple-element.682) | copy-start | bytes 196612
  346.5 10.9 %copy-start.83 = (f32[1,16,1024]{2,1,0:T(8,128)S(1)}, f32[1,16,1024]{2,1,0:T(8,128)}, u32[]{:S(2)}) copy-start(f32[1,16,1024]{2,1,0:T(8,128)} %get-tuple-element.681) | copy-start | bytes 196612
  410.9 5.0 collective-permute-start.6
  410.9 4.1 collective-permute-start.7
  453.9 20.2 %copy-start.404 = (pred[8]{0:T(512)(128)(4,1)S(1)}, pred[8]{0:T(512)(128)(4,1)}, u32[]{:S(2)}) copy-start(pred[8]{0:T(512)(128)(4,1)} %get-tuple-element.651) | copy-start | bytes 28
  453.9 15.4 %all-to-all-start.3 = ((f32[16,1,2880]{2,1,0:T(1,128)}), f32[16,1,2880]{2,1,0:T(1,128)S(1)}, u32[]{:S(2)}, u32[]{:S(2)}) async-start(f32[16,1,2880]{2,1,0:T(1,128)} %copy.749), calls=%async_computation.3 | async-start | bytes 376832 | tf_op jit(solution)/shard_map/all_to_all | solution.py:149
  461.5 12.9 %copy-start.414 = (s32[5]{0:T(128)S(1)}, s32[5]{0:T(128)}, u32[]{:S(2)}) copy-start(s32[5]{0:T(128)} %constant.1290) | copy-start | bytes 64
  469.3 35.7 %all-to-all-start.5 = ((s32[16,1,8]{2,1,0:T(1,128)}), s32[16,1,8]{2,1,0:T(1,128)S(1)}, u32[]{:S(2)}, u32[]{:S(2)}) async-start(s32[16,1,8]{2,1,0:T(1,128)} %bitcast.352), calls=%async_computation.5 | async-start | bytes 16384 | tf_op jit(solution)/shard_map/all_to_all | solution.py:317
  502.8 17.4 %copy-start.370 = (bf16[256,64]{0,1:T(8,128)(2,1)S(1)}, bf16[256,64]{0,1:T(8,128)(2,1)}, u32[]{:S(2)}) copy-start(bf16[256,64]{0,1:T(8,128)(2,1)} %get-tuple-element.1085) | copy-start | bytes 98308
  502.8 17.3 %copy-start.371 = (bf16[256,64]{0,1:T(8,128)(2,1)S(1)}, bf16[256,64]{0,1:T(8,128)(2,1)}, u32[]{:S(2)}) copy-start(bf16[256,64]{0,1:T(8,128)(2,1)} %get-tuple-element.1086) | copy-start | bytes 98308
  503.2 19.2 %copy-start.265 = (f32[3,512]{1,0:T(4,128)S(1)}, f32[3,512]{1,0:T(4,128)}, u32[]{:S(2)}) copy-start(f32[3,512]{1,0:T(4,128)} %param.149) | copy-start | bytes 18436
  503.2 19.2 %copy-start.307 = (bf16[128,3]{0,1:T(4,128)(2,1)S(1)}, bf16[128,3]{0,1:T(4,128)(2,1)}, u32[]{:S(2)}) copy-start(bf16[128,3]{0,1:T(4,128)(2,1)} %reshape.9282) | copy-start | bytes 2308
  505.0 14.8 %all-to-all-start.4 = ((bf16[16,8,512]{2,1,0:T(8,128)(2,1)}), bf16[16,8,512]{2,1,0:T(8,128)(2,1)S(1)}, u32[]{:S(2)}, u32[]{:S(2)}) async-start(bf16[16,8,512]{2,1,0:T(8,128)(2,1)} %bitcast_select_fusion), calls=%async_computation.4 | async-start | bytes 262144 | tf_op jit(solution)/shard_map/all_to_all | solution.py:316
  512.0 154.8 %reduce-scatter.2.cloned.1.call-start = ((), (), s32[]{:S(2)}) async-start(), calls=%async_computation.7 | async-start | bytes 278528 | tf_op jit(solution)/shard_map/reduce_scatter | solution.py:331
  (399 other events, 2271.9 us)
Sparse Core Ops, SparseCore 0:
  592.5 74.2 reduce-scatter.1
where the time goes:
time: 686 us; the launch traced here: 674 us
  local copies, waits for them, and re-layouts  360 us (52%)
  other arithmetic  153 us (22%)
  waiting for transfers between devices  87.7 us (13%)
  starting transfers between devices  43.1 us (6%)
  between operations  22.8 us (3%)
    reduce_scatter x1, waiting for transfers between devices, body(): lax.psum_scatter(partial_value, 'blk', scatter_dimension=0, tiled=True)  74.4 us
    reduce_sum x4, other arithmetic, radiate(): real_part = jnp.sum(weight_real * cosine + weight_imag * sine_part, axis=0)  67.3 us
    slice x96, local copies, waits for them, and re-layouts, stream_merged(): jnp.roll(widened[number, begin:begin + slab_depth], shift_y * BS + shift_...  63.9 us
    unnamed x110, other arithmetic  53.2 us
    concatenate x8, local copies, waits for them, and re-layouts, body(): widened = jnp.concatenate([lower_plane, collided, upper_plane], axis=1)  50.4 us
    another operation x120, local copies, waits for them, and re-layouts, stream_merged(): jnp.tile(row_values, (1, BS))  48.2 us
    reshape x80, local copies, waits for them, and re-layouts, stream_merged(): jnp.repeat(column_values, BS, axis=-1)  47.6 us
    unnamed x979, local copies, waits for them, and re-layouts  44.4 us
  transfers between devices with their start and end apart: 15, of which 3 were waited for; matrix products, arithmetic and copies ran while one was open for 14% of the time, Pallas kernels for 0%

commit v1 on v0

--- a/solution.py
+++ b/solution.py
@@ -41,6 +41,18 @@
 sound_speed = 0.5
 
 
+def cut_along(x, dim, size):
+    shape = x.shape
+    blocks = x.reshape(*shape[:dim], size, shape[dim] // size, *shape[dim + 1 :])
+    return jnp.moveaxis(blocks, dim, 0)
+
+
+def in_order(blocks, dim):
+    blocks = jnp.moveaxis(blocks, 0, dim)
+    shape = blocks.shape
+    return blocks.reshape(*shape[:dim], shape[dim] * shape[dim + 1], *shape[dim + 2 :])
+
+
 def padded(block, sides, width):
     for axis, dim in sides:
         count = lax.axis_size(axis)
@@ -146,9 +158,15 @@
         ]
     ).reshape(8, -1)
     targets = jnp.concatenate([block_faces, block_edges])
-    received = lax.all_to_all(
-        place_pieces(outgoing, targets, blocks), "blk", split_axis=0, concat_axis=0, tiled=True
-    )
+    value = place_pieces(outgoing, targets, blocks)
+    length, position = (lax.axis_size("blk"), lax.axis_index("blk"))
+    parts_2 = cut_along(value, 0, length)
+    gathered = [parts_2[position]]
+    for hop in range(1, length):
+        sent = parts_2[position ^ hop]
+        gathered.append(lax.ppermute(sent, "blk", [(i_2, i_2 ^ hop) for i_2 in range(length)]))
+    parts_2 = jnp.stack(gathered)[position ^ jnp.arange(length)]
+    received = in_order(parts_2, 0)
     chosen = jnp.take(received, targets, axis=0).reshape(8, 5, depth_x, BS)
     below_plane = spread_pops(chosen[0], y_upward, (19, depth_x, BS))
     above_plane = spread_pops(chosen[1], y_downward, (19, depth_x, BS))

time: 686 us -> 807 us (1.18)
  starting transfers between devices: 43.1 us -> 122 us
  other arithmetic: 153 us -> 179 us
  local copies, waits for them, and re-layouts: 360 us -> 381 us
    ppermute x0 -> x60, starting transfers between devices: none -> 107 us  [direct_halo(): lax.ppermute(sent, 'blk', [(i_2, i_2 ^ hop) for i_2 in range(length)])]
    all_to_all x4 -> x0, starting transfers between devices: 29.8 us -> none  [direct_halo(): lax.all_to_all(place_pieces(outgoing, targets, blocks), 'blk', split_axis...]
    unnamed x110, other arithmetic: 53.2 us -> 77.5 us
    another operation x20 -> x24, local copies, waits for them, and re-layouts: 0.3 us -> 8.49 us  [the longest x4 5.91 us: direct_halo(): parts_2 = jnp.stack(gathered)[position ^ jnp.arange(length)]]
    unnamed x979 -> x947, local copies, waits for them, and re-layouts: 44.4 us -> 46.3 us
  transfers between devices with their start and end apart: 15 -> 71, of which waited for: 3 -> 5; matrix products, arithmetic and copies ran while one was open for 14% -> 61% of each run, Pallas kernels for 0% -> 0%
where the time goes in v1:
time: 807 us; the launch traced here: 797 us
  local copies, waits for them, and re-layouts  381 us (47%)
  other arithmetic  179 us (22%)
  starting transfers between devices  122 us (15%)
  waiting for transfers between devices  83.6 us (10%)
  between operations  22.7 us (3%)
    ppermute x60, starting transfers between devices, direct_halo(): lax.ppermute(sent, 'blk', [(i_2, i_2 ^ hop) for i_2 in range(length)])  107 us
    unnamed x110, other arithmetic  77.5 us
    reduce_scatter x1, waiting for transfers between devices, body(): lax.psum_scatter(partial_value, 'blk', scatter_dimension=0, tiled=True)  74.4 us
    reduce_sum x4, other arithmetic, radiate(): real_part = jnp.sum(weight_real * cosine + weight_imag * sine_part, axis=0)  67.3 us
    slice x96, local copies, waits for them, and re-layouts, stream_merged(): jnp.roll(widened[number, begin:begin + slab_depth], shift_y * BS + shift_...  64 us
    concatenate x8, local copies, waits for them, and re-layouts, body(): widened = jnp.concatenate([lower_plane, collided, upper_plane], axis=1)  51.5 us
    another operation x120, local copies, waits for them, and re-layouts, stream_merged(): jnp.tile(row_values, (1, BS))  48.1 us
    reshape x80, local copies, waits for them, and re-layouts, stream_merged(): jnp.repeat(column_values, BS, axis=-1)  47.6 us
  transfers between devices with their start and end apart: 71, of which 5 were waited for; matrix products, arithmetic and copies ran while one was open for 61% of the time, Pallas kernels for 0%

profile of v1, /device:TPU:0, one launch (start us, length us, event | category | flops | bytes accessed | tf_op | source)
XLA Modules:
  0.0 797.2 jit_solution(8357687828716666496)
XLA Ops:
  12.4 8.4 %all-to-all-start.1 = ((s32[16,1,8]{2,1,0:T(1,128)}), s32[16,1,8]{2,1,0:T(1,128)}, u32[]{:S(2)}, u32[]{:S(2)}) async-start(s32[16,1,8]{2,1,0:T(1,128)} %bitcast.417), calls=%async_computation.1 | async-start | bytes 16384 | tf_op jit(solution)/shard_map/all_to_all | solution.py:335
  66.6 5.4 copy.660
  72.0 7.4 copy.656
  80.3 2.7 gather_fusion.4
  82.9 2.7 gather_fusion.3
  92.0 5.5 collective-permute-start.16
  98.1 3.1 collective-permute-start.14
  111.7 4.3 collective-permute-start.11
  116.2 2.4 collective-permute-start.9
  118.5 3.2 collective-permute-start.8
  124.6 2.8 collective-permute-start.4
  226.8 5.6 copy.682
  232.4 3.3 gather_fusion.10
  235.8 3.3 gather_fusion.9
  239.1 7.4 copy.678
  254.9 5.5 collective-permute-start.33
  261.2 3.0 collective-permute-start.31
  274.2 4.8 collective-permute-start.28
  279.2 2.3 collective-permute-start.26
  281.5 3.2 collective-permute-start.25
  287.5 2.8 collective-permute-start.21
  389.6 5.4 copy.704
  395.0 3.3 gather_fusion.16
  398.4 3.3 gather_fusion.15
  401.7 7.4 copy.700
  417.5 5.5 collective-permute-start.50
  423.7 2.9 collective-permute-start.48
  436.8 4.9 collective-permute-start.45
  444.1 3.1 collective-permute-start.42
  450.1 2.7 collective-permute-start.38
  542.0 5.4 copy.726
  547.4 2.7 gather_fusion.22
  550.1 2.7 gather_fusion.21
  552.7 7.5 copy.722
  565.7 5.4 collective-permute-start.67
  571.9 2.8 collective-permute-start.65
  576.2 4.9 collective-permute-start.62
  581.3 2.3 collective-permute-start.60
  583.6 3.0 collective-permute-start.59
  590.1 2.7 collective-permute-start.55
  630.2 5.3 all-to-all-start
  637.2 6.1 all-to-all-done
  645.6 69.2 %while.46 = (s32[]{:T(128)}, f32[512,128]{0,1:T(8,128)S(1)}, bf16[3,128]{1,0:T(4,128)(2,1)S(1)}, f32[3,512]{1,0:T(4,128)S(1)}, bf16[3,128]{1,0:T(4,128)(2,1)S(1)...) while((s32[]{:T(128)}, f32[512,128]{0,1:T(8,128)S(1)}, ...), condition=%wide.region_46.49_spmd.clone, body=%wide.region_41.48_spmd.clone.sunk | while | flops 16179527 | bytes 1860141 | solution.py:241
  646.0 16.8 %fusion.304 = (f32[64,512]{1,0:T(8,128)S(1)}, f32[64,512]{1,0:T(8,128)S(1)}) fusion(f32[32,64]{1,0:T(8,128)S(1)} %get-tuple-element.1239, f32[32,64]{1,0:T(8,128)S(1)} %get-tuple-element.1240, f32[32,512]{1,0:T(8,128)S(1)} %get-tuple-element.1245, f32[64]{0:T(128)S(1)} %add_multiply_fusion.3, f32[32,64]{1,0:T(8,128)S(1)} %get-tuple-element.1246, ...), kind=kLoop, calls=%fused_computation.65.clone.1 | loop fusion | flops 15663104 | bytes 491776 | tf_op jit(solution)/shard_map/while/body/eval_jaxpr/reduce_sum | solution.py:218
  663.3 16.8 %fusion.304 = (f32[64,512]{1,0:T(8,128)S(1)}, f32[64,512]{1,0:T(8,128)S(1)}) fusion(f32[32,64]{1,0:T(8,128)S(1)} %get-tuple-element.1239, f32[32,64]{1,0:T(8,128)S(1)} %get-tuple-element.1240, f32[32,512]{1,0:T(8,128)S(1)} %get-tuple-element.1245, f32[64]{0:T(128)S(1)} %add_multiply_fusion.3, f32[32,64]{1,0:T(8,128)S(1)} %get-tuple-element.1246, ...), kind=kLoop, calls=%fused_computation.65.clone.1 | loop fusion | flops 15663104 | bytes 491776 | tf_op jit(solution)/shard_map/while/body/eval_jaxpr/reduce_sum | solution.py:218
  680.6 16.8 %fusion.304 = (f32[64,512]{1,0:T(8,128)S(1)}, f32[64,512]{1,0:T(8,128)S(1)}) fusion(f32[32,64]{1,0:T(8,128)S(1)} %get-tuple-element.1239, f32[32,64]{1,0:T(8,128)S(1)} %get-tuple-element.1240, f32[32,512]{1,0:T(8,128)S(1)} %get-tuple-element.1245, f32[64]{0:T(128)S(1)} %add_multiply_fusion.3, f32[32,64]{1,0:T(8,128)S(1)} %get-tuple-element.1246, ...), kind=kLoop, calls=%fused_computation.65.clone.1 | loop fusion | flops 15663104 | bytes 491776 | tf_op jit(solution)/shard_map/while/body/eval_jaxpr/reduce_sum | solution.py:218
  697.9 16.8 %fusion.304 = (f32[64,512]{1,0:T(8,128)S(1)}, f32[64,512]{1,0:T(8,128)S(1)}) fusion(f32[32,64]{1,0:T(8,128)S(1)} %get-tuple-element.1239, f32[32,64]{1,0:T(8,128)S(1)} %get-tuple-element.1240, f32[32,512]{1,0:T(8,128)S(1)} %get-tuple-element.1245, f32[64]{0:T(128)S(1)} %add_multiply_fusion.3, f32[32,64]{1,0:T(8,128)S(1)} %get-tuple-element.1246, ...), kind=kLoop, calls=%fused_computation.65.clone.1 | loop fusion | flops 15663104 | bytes 491776 | tf_op jit(solution)/shard_map/while/body/eval_jaxpr/reduce_sum | solution.py:218
  715.7 74.4 %reduce-scatter.2.cloned.1.call-done = f32[32,128]{1,0:T(8,128)} async-done(((f32[512,128]{1,0:T(8,128)}), f32[32,128]{1,0:T(8,128)}) %reduce-scatter.2.cloned.1.call-update) | async-done | bytes 16400 | tf_op jit(solution)/shard_map/reduce_scatter | solution.py:349
  (1890 shorter events, 454.2 us)
Async XLA Ops:
  12.4 617.8 %all-to-all-start.1 = ((s32[16,1,8]{2,1,0:T(1,128)}), s32[16,1,8]{2,1,0:T(1,128)}, u32[]{:S(2)}, u32[]{:S(2)}) async-start(s32[16,1,8]{2,1,0:T(1,128)} %bitcast.417), calls=%async_computation.1 | async-start | bytes 16384 | tf_op jit(solution)/shard_map/all_to_all | solution.py:335
  25.6 16.7 %collective-permute-start = (f32[10,1,1024]{2,1,0:T(1,128)S(1)}, f32[10,1,1024]{2,1,0:T(1,128)S(1)}, u32[]{:S(2)}, u32[]{:S(2)}) collective-permute-start(f32[10,1,1024]{2,1,0:T(1,128)S(1)} %get-tuple-element.752), channel_id=1, source_target_pairs={{0,1},{1,0},{2,3},{3,2},{4,5},{5,4},{6,7},{7,6},{8,9},{9,8},{10,11... | collective-permute-start | bytes 122888 | tf_op jit(solution)/shard_map/ppermute | solution.py:62
  25.7 15.7 %collective-permute-start.1 = (f32[10,1,1024]{2,1,0:T(1,128)S(1)}, f32[10,1,1024]{2,1,0:T(1,128)S(1)}, u32[]{:S(2)}, u32[]{:S(2)}) collective-permute-start(f32[10,1,1024]{2,1,0:T(1,128)S(1)} %get-tuple-element.753), channel_id=1, source_target_pairs={{1,0},{0,1},{3,2},{2,3},{5,4},{4,5},{7,6},{6,7},{9,8},{8,9},{11,10... | collective-permute-start | bytes 122888 | tf_op jit(solution)/shard_map/ppermute | solution.py:65
  92.0 19.7 %collective-permute-start.16 = (f32[1,2880]{1,0:T(1,128)S(1)}, f32[1,2880]{1,0:T(1,128)S(1)}, u32[]{:S(2)}, u32[]{:S(2)}) collective-permute-start(f32[1,2880]{1,0:T(1,128)S(1)} %get-tuple-element.898), channel_id=1, source_target_pairs={{0,30},{2,28},{4,26},{6,24},{8,22},{10,20},{12,18},{14,16},{16,14}... | collective-permute-start | bytes 34568 | tf_op jit(solution)/shard_map/ppermute | solution.py:167
  97.5 18.5 %collective-permute-start.15 = (f32[1,2880]{1,0:T(1,128)S(1)}, f32[1,2880]{1,0:T(1,128)S(1)}, u32[]{:S(2)}, u32[]{:S(2)}) collective-permute-start(f32[1,2880]{1,0:T(1,128)S(1)} %get-tuple-element.899), channel_id=1, source_target_pairs={{0,28},{2,30},{4,24},{6,26},{8,20},{10,22},{12,16},{14,18},{16,12}... | collective-permute-start | bytes 34568 | tf_op jit(solution)/shard_map/ppermute | solution.py:167
  98.1 18.0 %collective-permute-start.14 = (f32[1,2880]{1,0:T(1,128)S(1)}, f32[1,2880]{1,0:T(1,128)S(1)}, u32[]{:S(2)}, u32[]{:S(2)}) collective-permute-start(f32[1,2880]{1,0:T(1,128)S(1)} %get-tuple-element.900), channel_id=1, source_target_pairs={{0,26},{2,24},{4,30},{6,28},{8,18},{10,16},{12,22},{14,20},{16,10}... | collective-permute-start | bytes 34568 | tf_op jit(solution)/shard_map/ppermute | solution.py:167
  101.2 17.3 %collective-permute-start.13 = (f32[1,2880]{1,0:T(1,128)S(1)}, f32[1,2880]{1,0:T(1,128)S(1)}, u32[]{:S(2)}, u32[]{:S(2)}) collective-permute-start(f32[1,2880]{1,0:T(1,128)S(1)} %get-tuple-element.901), channel_id=1, source_target_pairs={{0,24},{2,26},{4,28},{6,30},{8,16},{10,18},{12,20},{14,22},{16,8},... | collective-permute-start | bytes 34568 | tf_op jit(solution)/shard_map/ppermute | solution.py:167
  101.5 20.2 %collective-permute-start.12 = (f32[1,2880]{1,0:T(1,128)S(1)}, f32[1,2880]{1,0:T(1,128)S(1)}, u32[]{:S(2)}, u32[]{:S(2)}) collective-permute-start(f32[1,2880]{1,0:T(1,128)S(1)} %get-tuple-element.902), channel_id=1, source_target_pairs={{0,22},{2,20},{4,18},{6,16},{8,30},{10,28},{12,26},{14,24},{16,6},... | collective-permute-start | bytes 34568 | tf_op jit(solution)/shard_map/ppermute | solution.py:167
  111.7 11.2 %collective-permute-start.11 = (f32[1,2880]{1,0:T(1,128)S(1)}, f32[1,2880]{1,0:T(1,128)S(1)}, u32[]{:S(2)}, u32[]{:S(2)}) collective-permute-start(f32[1,2880]{1,0:T(1,128)S(1)} %get-tuple-element.903), channel_id=1, source_target_pairs={{0,20},{2,22},{4,16},{6,18},{8,28},{10,30},{12,24},{14,26},{16,4},... | collective-permute-start | bytes 34568 | tf_op jit(solution)/shard_map/ppermute | solution.py:167
  118.5 8.8 %collective-permute-start.8 = (f32[1,2880]{1,0:T(1,128)S(1)}, f32[1,2880]{1,0:T(1,128)S(1)}, u32[]{:S(2)}, u32[]{:S(2)}) collective-permute-start(f32[1,2880]{1,0:T(1,128)S(1)} %get-tuple-element.906), channel_id=1, source_target_pairs={{0,14},{2,12},{4,10},{6,8},{8,6},{10,4},{12,2},{14,0},{16,30},{18,... | collective-permute-start | bytes 34568 | tf_op jit(solution)/shard_map/ppermute | solution.py:167
  122.9 16.0 %collective-permute-start.6 = (f32[1,2880]{1,0:T(1,128)S(1)}, f32[1,2880]{1,0:T(1,128)S(1)}, u32[]{:S(2)}, u32[]{:S(2)}) collective-permute-start(f32[1,2880]{1,0:T(1,128)S(1)} %get-tuple-element.908), channel_id=1, source_target_pairs={{0,10},{2,8},{4,14},{6,12},{8,2},{10,0},{12,6},{14,4},{16,26},{18,... | collective-permute-start | bytes 34568 | tf_op jit(solution)/shard_map/ppermute | solution.py:167
  123.9 15.1 %collective-permute-start.5 = (f32[1,2880]{1,0:T(1,128)S(1)}, f32[1,2880]{1,0:T(1,128)S(1)}, u32[]{:S(2)}, u32[]{:S(2)}) collective-permute-start(f32[1,2880]{1,0:T(1,128)S(1)} %get-tuple-element.909), channel_id=1, source_target_pairs={{0,8},{2,10},{4,12},{6,14},{8,0},{10,2},{12,4},{14,6},{16,24},{18,... | collective-permute-start | bytes 34568 | tf_op jit(solution)/shard_map/ppermute | solution.py:167
  124.6 14.4 %collective-permute-start.4 = (f32[1,2880]{1,0:T(1,128)S(1)}, f32[1,2880]{1,0:T(1,128)S(1)}, u32[]{:S(2)}, u32[]{:S(2)}) collective-permute-start(f32[1,2880]{1,0:T(1,128)S(1)} %get-tuple-element.910), channel_id=1, source_target_pairs={{0,6},{2,4},{4,2},{6,0},{8,14},{10,12},{12,10},{14,8},{16,22},{18,... | collective-permute-start | bytes 34568 | tf_op jit(solution)/shard_map/ppermute | solution.py:167
  127.3 11.7 %collective-permute-start.3 = (f32[1,2880]{1,0:T(1,128)S(1)}, f32[1,2880]{1,0:T(1,128)S(1)}, u32[]{:S(2)}, u32[]{:S(2)}) collective-permute-start(f32[1,2880]{1,0:T(1,128)S(1)} %get-tuple-element.911), channel_id=1, source_target_pairs={{0,4},{2,6},{4,0},{6,2},{8,12},{10,14},{12,8},{14,10},{16,20},{18,... | collective-permute-start | bytes 34568 | tf_op jit(solution)/shard_map/ppermute | solution.py:167
  128.0 11.1 %collective-permute-start.2 = (f32[1,2880]{1,0:T(1,128)S(1)}, f32[1,2880]{1,0:T(1,128)S(1)}, u32[]{:S(2)}, u32[]{:S(2)}) collective-permute-start(f32[1,2880]{1,0:T(1,128)S(1)} %get-tuple-element.912), channel_id=1, source_target_pairs={{0,2},{2,0},{4,6},{6,4},{8,10},{10,8},{12,14},{14,12},{16,18},{18,... | collective-permute-start | bytes 34568 | tf_op jit(solution)/shard_map/ppermute | solution.py:167
  254.9 19.3 %collective-permute-start.33 = (f32[1,2880]{1,0:T(1,128)S(1)}, f32[1,2880]{1,0:T(1,128)S(1)}, u32[]{:S(2)}, u32[]{:S(2)}) collective-permute-start(f32[1,2880]{1,0:T(1,128)S(1)} %get-tuple-element.882), channel_id=1, source_target_pairs={{0,30},{2,28},{4,26},{6,24},{8,22},{10,20},{12,18},{14,16},{16,14}... | collective-permute-start | bytes 34568 | tf_op jit(solution)/shard_map/ppermute | solution.py:167
  260.5 18.6 %collective-permute-start.32 = (f32[1,2880]{1,0:T(1,128)S(1)}, f32[1,2880]{1,0:T(1,128)S(1)}, u32[]{:S(2)}, u32[]{:S(2)}) collective-permute-start(f32[1,2880]{1,0:T(1,128)S(1)} %get-tuple-element.883), channel_id=1, source_target_pairs={{0,28},{2,30},{4,24},{6,26},{8,20},{10,22},{12,16},{14,18},{16,12}... | collective-permute-start | bytes 34568 | tf_op jit(solution)/shard_map/ppermute | solution.py:167
  261.2 18.1 %collective-permute-start.31 = (f32[1,2880]{1,0:T(1,128)S(1)}, f32[1,2880]{1,0:T(1,128)S(1)}, u32[]{:S(2)}, u32[]{:S(2)}) collective-permute-start(f32[1,2880]{1,0:T(1,128)S(1)} %get-tuple-element.884), channel_id=1, source_target_pairs={{0,26},{2,24},{4,30},{6,28},{8,18},{10,16},{12,22},{14,20},{16,10}... | collective-permute-start | bytes 34568 | tf_op jit(solution)/shard_map/ppermute | solution.py:167
  264.1 17.4 %collective-permute-start.30 = (f32[1,2880]{1,0:T(1,128)S(1)}, f32[1,2880]{1,0:T(1,128)S(1)}, u32[]{:S(2)}, u32[]{:S(2)}) collective-permute-start(f32[1,2880]{1,0:T(1,128)S(1)} %get-tuple-element.885), channel_id=1, source_target_pairs={{0,24},{2,26},{4,28},{6,30},{8,16},{10,18},{12,20},{14,22},{16,8},... | collective-permute-start | bytes 34568 | tf_op jit(solution)/shard_map/ppermute | solution.py:167
  264.4 20.2 %collective-permute-start.29 = (f32[1,2880]{1,0:T(1,128)S(1)}, f32[1,2880]{1,0:T(1,128)S(1)}, u32[]{:S(2)}, u32[]{:S(2)}) collective-permute-start(f32[1,2880]{1,0:T(1,128)S(1)} %get-tuple-element.886), channel_id=1, source_target_pairs={{0,22},{2,20},{4,18},{6,16},{8,30},{10,28},{12,26},{14,24},{16,6},... | collective-permute-start | bytes 34568 | tf_op jit(solution)/shard_map/ppermute | solution.py:167
  274.2 11.7 %collective-permute-start.28 = (f32[1,2880]{1,0:T(1,128)S(1)}, f32[1,2880]{1,0:T(1,128)S(1)}, u32[]{:S(2)}, u32[]{:S(2)}) collective-permute-start(f32[1,2880]{1,0:T(1,128)S(1)} %get-tuple-element.887), channel_id=1, source_target_pairs={{0,20},{2,22},{4,16},{6,18},{8,28},{10,30},{12,24},{14,26},{16,4},... | collective-permute-start | bytes 34568 | tf_op jit(solution)/shard_map/ppermute | solution.py:167
  281.5 8.8 %collective-permute-start.25 = (f32[1,2880]{1,0:T(1,128)S(1)}, f32[1,2880]{1,0:T(1,128)S(1)}, u32[]{:S(2)}, u32[]{:S(2)}) collective-permute-start(f32[1,2880]{1,0:T(1,128)S(1)} %get-tuple-element.890), channel_id=1, source_target_pairs={{0,14},{2,12},{4,10},{6,8},{8,6},{10,4},{12,2},{14,0},{16,30},{18,... | collective-permute-start | bytes 34568 | tf_op jit(solution)/shard_map/ppermute | solution.py:167
  285.9 16.0 %collective-permute-start.23 = (f32[1,2880]{1,0:T(1,128)S(1)}, f32[1,2880]{1,0:T(1,128)S(1)}, u32[]{:S(2)}, u32[]{:S(2)}) collective-permute-start(f32[1,2880]{1,0:T(1,128)S(1)} %get-tuple-element.892), channel_id=1, source_target_pairs={{0,10},{2,8},{4,14},{6,12},{8,2},{10,0},{12,6},{14,4},{16,26},{18,... | collective-permute-start | bytes 34568 | tf_op jit(solution)/shard_map/ppermute | solution.py:167
  286.9 15.1 %collective-permute-start.22 = (f32[1,2880]{1,0:T(1,128)S(1)}, f32[1,2880]{1,0:T(1,128)S(1)}, u32[]{:S(2)}, u32[]{:S(2)}) collective-permute-start(f32[1,2880]{1,0:T(1,128)S(1)} %get-tuple-element.893), channel_id=1, source_target_pairs={{0,8},{2,10},{4,12},{6,14},{8,0},{10,2},{12,4},{14,6},{16,24},{18,... | collective-permute-start | bytes 34568 | tf_op jit(solution)/shard_map/ppermute | solution.py:167
  287.5 14.5 %collective-permute-start.21 = (f32[1,2880]{1,0:T(1,128)S(1)}, f32[1,2880]{1,0:T(1,128)S(1)}, u32[]{:S(2)}, u32[]{:S(2)}) collective-permute-start(f32[1,2880]{1,0:T(1,128)S(1)} %get-tuple-element.894), channel_id=1, source_target_pairs={{0,6},{2,4},{4,2},{6,0},{8,14},{10,12},{12,10},{14,8},{16,22},{18,... | collective-permute-start | bytes 34568 | tf_op jit(solution)/shard_map/ppermute | solution.py:167
  290.3 11.7 %collective-permute-start.20 = (f32[1,2880]{1,0:T(1,128)S(1)}, f32[1,2880]{1,0:T(1,128)S(1)}, u32[]{:S(2)}, u32[]{:S(2)}) collective-permute-start(f32[1,2880]{1,0:T(1,128)S(1)} %get-tuple-element.895), channel_id=1, source_target_pairs={{0,4},{2,6},{4,0},{6,2},{8,12},{10,14},{12,8},{14,10},{16,20},{18,... | collective-permute-start | bytes 34568 | tf_op jit(solution)/shard_map/ppermute | solution.py:167
  291.0 11.1 %collective-permute-start.19 = (f32[1,2880]{1,0:T(1,128)S(1)}, f32[1,2880]{1,0:T(1,128)S(1)}, u32[]{:S(2)}, u32[]{:S(2)}) collective-permute-start(f32[1,2880]{1,0:T(1,128)S(1)} %get-tuple-element.896), channel_id=1, source_target_pairs={{0,2},{2,0},{4,6},{6,4},{8,10},{10,8},{12,14},{14,12},{16,18},{18,... | collective-permute-start | bytes 34568 | tf_op jit(solution)/shard_map/ppermute | solution.py:167
  417.5 19.2 %collective-permute-start.50 = (f32[1,2880]{1,0:T(1,128)S(1)}, f32[1,2880]{1,0:T(1,128)S(1)}, u32[]{:S(2)}, u32[]{:S(2)}) collective-permute-start(f32[1,2880]{1,0:T(1,128)S(1)} %get-tuple-element.866), channel_id=1, source_target_pairs={{0,30},{2,28},{4,26},{6,24},{8,22},{10,20},{12,18},{14,16},{16,14}... | collective-permute-start | bytes 34568 | tf_op jit(solution)/shard_map/ppermute | solution.py:167
  423.0 18.7 %collective-permute-start.49 = (f32[1,2880]{1,0:T(1,128)S(1)}, f32[1,2880]{1,0:T(1,128)S(1)}, u32[]{:S(2)}, u32[]{:S(2)}) collective-permute-start(f32[1,2880]{1,0:T(1,128)S(1)} %get-tuple-element.867), channel_id=1, source_target_pairs={{0,28},{2,30},{4,24},{6,26},{8,20},{10,22},{12,16},{14,18},{16,12}... | collective-permute-start | bytes 34568 | tf_op jit(solution)/shard_map/ppermute | solution.py:167
  423.7 18.1 %collective-permute-start.48 = (f32[1,2880]{1,0:T(1,128)S(1)}, f32[1,2880]{1,0:T(1,128)S(1)}, u32[]{:S(2)}, u32[]{:S(2)}) collective-permute-start(f32[1,2880]{1,0:T(1,128)S(1)} %get-tuple-element.868), channel_id=1, source_target_pairs={{0,26},{2,24},{4,30},{6,28},{8,18},{10,16},{12,22},{14,20},{16,10}... | collective-permute-start | bytes 34568 | tf_op jit(solution)/shard_map/ppermute | solution.py:167
  426.6 17.5 %collective-permute-start.47 = (f32[1,2880]{1,0:T(1,128)S(1)}, f32[1,2880]{1,0:T(1,128)S(1)}, u32[]{:S(2)}, u32[]{:S(2)}) collective-permute-start(f32[1,2880]{1,0:T(1,128)S(1)} %get-tuple-element.869), channel_id=1, source_target_pairs={{0,24},{2,26},{4,28},{6,30},{8,16},{10,18},{12,20},{14,22},{16,8},... | collective-permute-start | bytes 34568 | tf_op jit(solution)/shard_map/ppermute | solution.py:167
  427.0 20.2 %collective-permute-start.46 = (f32[1,2880]{1,0:T(1,128)S(1)}, f32[1,2880]{1,0:T(1,128)S(1)}, u32[]{:S(2)}, u32[]{:S(2)}) collective-permute-start(f32[1,2880]{1,0:T(1,128)S(1)} %get-tuple-element.870), channel_id=1, source_target_pairs={{0,22},{2,20},{4,18},{6,16},{8,30},{10,28},{12,26},{14,24},{16,6},... | collective-permute-start | bytes 34568 | tf_op jit(solution)/shard_map/ppermute | solution.py:167
  436.8 11.8 %collective-permute-start.45 = (f32[1,2880]{1,0:T(1,128)S(1)}, f32[1,2880]{1,0:T(1,128)S(1)}, u32[]{:S(2)}, u32[]{:S(2)}) collective-permute-start(f32[1,2880]{1,0:T(1,128)S(1)} %get-tuple-element.871), channel_id=1, source_target_pairs={{0,20},{2,22},{4,16},{6,18},{8,28},{10,30},{12,24},{14,26},{16,4},... | collective-permute-start | bytes 34568 | tf_op jit(solution)/shard_map/ppermute | solution.py:167
  444.1 8.8 %collective-permute-start.42 = (f32[1,2880]{1,0:T(1,128)S(1)}, f32[1,2880]{1,0:T(1,128)S(1)}, u32[]{:S(2)}, u32[]{:S(2)}) collective-permute-start(f32[1,2880]{1,0:T(1,128)S(1)} %get-tuple-element.874), channel_id=1, source_target_pairs={{0,14},{2,12},{4,10},{6,8},{8,6},{10,4},{12,2},{14,0},{16,30},{18,... | collective-permute-start | bytes 34568 | tf_op jit(solution)/shard_map/ppermute | solution.py:167
  448.5 16.1 %collective-permute-start.40 = (f32[1,2880]{1,0:T(1,128)S(1)}, f32[1,2880]{1,0:T(1,128)S(1)}, u32[]{:S(2)}, u32[]{:S(2)}) collective-permute-start(f32[1,2880]{1,0:T(1,128)S(1)} %get-tuple-element.876), channel_id=1, source_target_pairs={{0,10},{2,8},{4,14},{6,12},{8,2},{10,0},{12,6},{14,4},{16,26},{18,... | collective-permute-start | bytes 34568 | tf_op jit(solution)/shard_map/ppermute | solution.py:167
  449.4 15.2 %collective-permute-start.39 = (f32[1,2880]{1,0:T(1,128)S(1)}, f32[1,2880]{1,0:T(1,128)S(1)}, u32[]{:S(2)}, u32[]{:S(2)}) collective-permute-start(f32[1,2880]{1,0:T(1,128)S(1)} %get-tuple-element.877), channel_id=1, source_target_pairs={{0,8},{2,10},{4,12},{6,14},{8,0},{10,2},{12,4},{14,6},{16,24},{18,... | collective-permute-start | bytes 34568 | tf_op jit(solution)/shard_map/ppermute | solution.py:167
  450.1 14.5 %collective-permute-start.38 = (f32[1,2880]{1,0:T(1,128)S(1)}, f32[1,2880]{1,0:T(1,128)S(1)}, u32[]{:S(2)}, u32[]{:S(2)}) collective-permute-start(f32[1,2880]{1,0:T(1,128)S(1)} %get-tuple-element.878), channel_id=1, source_target_pairs={{0,6},{2,4},{4,2},{6,0},{8,14},{10,12},{12,10},{14,8},{16,22},{18,... | collective-permute-start | bytes 34568 | tf_op jit(solution)/shard_map/ppermute | solution.py:167
  452.9 11.8 %collective-permute-start.37 = (f32[1,2880]{1,0:T(1,128)S(1)}, f32[1,2880]{1,0:T(1,128)S(1)}, u32[]{:S(2)}, u32[]{:S(2)}) collective-permute-start(f32[1,2880]{1,0:T(1,128)S(1)} %get-tuple-element.879), channel_id=1, source_target_pairs={{0,4},{2,6},{4,0},{6,2},{8,12},{10,14},{12,8},{14,10},{16,20},{18,... | collective-permute-start | bytes 34568 | tf_op jit(solution)/shard_map/ppermute | solution.py:167
  453.6 11.1 %collective-permute-start.36 = (f32[1,2880]{1,0:T(1,128)S(1)}, f32[1,2880]{1,0:T(1,128)S(1)}, u32[]{:S(2)}, u32[]{:S(2)}) collective-permute-start(f32[1,2880]{1,0:T(1,128)S(1)} %get-tuple-element.880), channel_id=1, source_target_pairs={{0,2},{2,0},{4,6},{6,4},{8,10},{10,8},{12,14},{14,12},{16,18},{18,... | collective-permute-start | bytes 34568 | tf_op jit(solution)/shard_map/ppermute | solution.py:167
  565.7 10.5 %collective-permute-start.67 = (f32[1,2880]{1,0:T(1,128)S(1)}, f32[1,2880]{1,0:T(1,128)S(1)}, u32[]{:S(2)}, u32[]{:S(2)}) collective-permute-start(f32[1,2880]{1,0:T(1,128)S(1)} %get-tuple-element.850), channel_id=1, source_target_pairs={{0,30},{2,28},{4,26},{6,24},{8,22},{10,20},{12,18},{14,16},{16,14}... | collective-permute-start | bytes 34568 | tf_op jit(solution)/shard_map/ppermute | solution.py:167
  571.1 10.0 %collective-permute-start.66 = (f32[1,2880]{1,0:T(1,128)S(1)}, f32[1,2880]{1,0:T(1,128)S(1)}, u32[]{:S(2)}, u32[]{:S(2)}) collective-permute-start(f32[1,2880]{1,0:T(1,128)S(1)} %get-tuple-element.851), channel_id=1, source_target_pairs={{0,28},{2,30},{4,24},{6,26},{8,20},{10,22},{12,16},{14,18},{16,12}... | collective-permute-start | bytes 34568 | tf_op jit(solution)/shard_map/ppermute | solution.py:167
  571.9 9.4 %collective-permute-start.65 = (f32[1,2880]{1,0:T(1,128)S(1)}, f32[1,2880]{1,0:T(1,128)S(1)}, u32[]{:S(2)}, u32[]{:S(2)}) collective-permute-start(f32[1,2880]{1,0:T(1,128)S(1)} %get-tuple-element.852), channel_id=1, source_target_pairs={{0,26},{2,24},{4,30},{6,28},{8,18},{10,16},{12,22},{14,20},{16,10}... | collective-permute-start | bytes 34568 | tf_op jit(solution)/shard_map/ppermute | solution.py:167
  574.7 8.9 %collective-permute-start.64 = (f32[1,2880]{1,0:T(1,128)S(1)}, f32[1,2880]{1,0:T(1,128)S(1)}, u32[]{:S(2)}, u32[]{:S(2)}) collective-permute-start(f32[1,2880]{1,0:T(1,128)S(1)} %get-tuple-element.853), channel_id=1, source_target_pairs={{0,24},{2,26},{4,28},{6,30},{8,16},{10,18},{12,20},{14,22},{16,8},... | collective-permute-start | bytes 34568 | tf_op jit(solution)/shard_map/ppermute | solution.py:167
  575.2 11.3 %collective-permute-start.63 = (f32[1,2880]{1,0:T(1,128)S(1)}, f32[1,2880]{1,0:T(1,128)S(1)}, u32[]{:S(2)}, u32[]{:S(2)}) collective-permute-start(f32[1,2880]{1,0:T(1,128)S(1)} %get-tuple-element.854), channel_id=1, source_target_pairs={{0,22},{2,20},{4,18},{6,16},{8,30},{10,28},{12,26},{14,24},{16,6},... | collective-permute-start | bytes 34568 | tf_op jit(solution)/shard_map/ppermute | solution.py:167
  576.2 12.3 %collective-permute-start.62 = (f32[1,2880]{1,0:T(1,128)S(1)}, f32[1,2880]{1,0:T(1,128)S(1)}, u32[]{:S(2)}, u32[]{:S(2)}) collective-permute-start(f32[1,2880]{1,0:T(1,128)S(1)} %get-tuple-element.855), channel_id=1, source_target_pairs={{0,20},{2,22},{4,16},{6,18},{8,28},{10,30},{12,24},{14,26},{16,4},... | collective-permute-start | bytes 34568 | tf_op jit(solution)/shard_map/ppermute | solution.py:167
  583.6 9.2 %collective-permute-start.59 = (f32[1,2880]{1,0:T(1,128)S(1)}, f32[1,2880]{1,0:T(1,128)S(1)}, u32[]{:S(2)}, u32[]{:S(2)}) collective-permute-start(f32[1,2880]{1,0:T(1,128)S(1)} %get-tuple-element.858), channel_id=1, source_target_pairs={{0,14},{2,12},{4,10},{6,8},{8,6},{10,4},{12,2},{14,0},{16,30},{18,... | collective-permute-start | bytes 34568 | tf_op jit(solution)/shard_map/ppermute | solution.py:167
  630.2 13.1 %all-to-all-start = ((bf16[16,8,512]{2,1,0:T(8,128)(2,1)}), bf16[16,8,512]{2,1,0:T(8,128)(2,1)S(1)}, u32[]{:S(2)}, u32[]{:S(2)}) async-start(bf16[16,8,512]{2,1,0:T(8,128)(2,1)} %bitcast_select_fusion), calls=%async_computation | async-start | bytes 262144 | tf_op jit(solution)/shard_map/all_to_all | solution.py:334
  635.5 154.6 %reduce-scatter.2.cloned.1.call-start = ((), (), s32[]{:S(2)}) async-start(), calls=%async_computation.3 | async-start | bytes 278528 | tf_op jit(solution)/shard_map/reduce_scatter | solution.py:349
  (441 other events, 3597.6 us)
Sparse Core Ops, SparseCore 0:
  715.8 74.2 reduce-scatter.1
